TPU v7x, 128 devices: a whole 4x4x4 slice. The times are simulated.
128 devices in a mesh: dp: 16 (over y, z), vocab: 8 (over x, core).
Axes of the slice: x: 4, y: 4, z: 4, core: 2. Of those that a mesh axis runs over, the one named last changes fastest.
Arguments:
- tokens: bfloat16 [2048, 7168], P('dp'), may hold values from -6 to 6
- expert_hidden: bfloat16 [2048, 8, 1024], P('dp'), may hold values from -6 to 6
- routes: int32 [2048, 8], P('dp'), may hold values from 0 to 63, all different within a row; in each aligned block of 16 rows (0 to 15, 16 to 31, ...) at most 3 rows name the same one
- route_weight: float32 [2048, 8], P('dp'), may hold values from 0.05 to 0.45
- expert_weight: bfloat16 [128, 512, 7168], P(('dp', 'vocab')), may hold values from -0.1875 to 0.1875
- norm_gain: float32 [7168], replicated, may hold values from 0.5 to 1.5
- head_weight: bfloat16 [7168, 114688], P(None, ('dp', 'vocab')), may hold values from -8 to 8
- targets: int32 [2048], P('dp'), may hold values from 0 to 114687
- rollout_logprob: float32 [2048], P('dp'), may hold values from -21 to -13
- advantages: float32 [2048], P('dp'), may hold values from -5 to 5
Outputs:
- layer_out: bfloat16 [2048, 7168], P('dp')
- token_logprob: float32 [2048], P('dp')
- token_loss: float32 [2048], P('dp')
Inputs may be any that keep to these rules, and one draw needn't show every extreme that they name: The 8 routes of a token name different experts; among the routes of one aligned block of 16 token rows, no expert is named more than 3 times.
All inputs are finite; a program needn't handle non-finite values.
Results may differ from a plain program's by a relative error of at most 0.02.
Values may be sent and summed in bfloat16 or wider, within the bound.
No kernel may reach another device: no remote copies, remote signals or barrier semaphores. Data moves between devices by JAX's collectives and lax.ppermute only.
A program may use at most 192 MiB of HBM per device.

v0:
```python
import jax
import jax.numpy as jnp
from jax import lax
from jax.sharding import Mesh
from jax.sharding import PartitionSpec as P

X = "vocab_0"
CORE = "vocab_1"
VOCAB = ("vocab_0", "vocab_1")
DP_VOCAB = ("dp_0", "dp_1", "vocab_0", "vocab_1")
DP = ("dp_0", "dp_1")
norm_epsilon = 1e-06
clip_low = 0.8
clip_high = 1.2
dual_bound = 3.0
bf16 = jnp.bfloat16
f32 = jnp.float32


def clipped_loss(logprob, rollout_logprob, advantages):
    ratio = jnp.exp(logprob - rollout_logprob)
    surrogate = jnp.minimum(ratio * advantages, jnp.clip(ratio, clip_low, clip_high) * advantages)
    bounded = jnp.where(
        advantages < 0.0, jnp.maximum(surrogate, dual_bound * advantages), surrogate
    )
    return -bounded


def dot(a, b):
    return jnp.dot(a, b, preferred_element_type=f32)


def swap_cores(x):
    return lax.ppermute(x, CORE, [(0, 1), (1, 0)])


def label_row(targets):
    digits = [targets // 128**k % 128 for k in range(3)]
    row = jnp.concatenate(digits + [jnp.zeros_like(targets)]).astype(bf16)
    return row[None]


def labels_of(rows):
    digits = rows.astype(f32).astype(jnp.int32).reshape(rows.shape[0], 4, 128)
    return digits[:, 0] + 128 * digits[:, 1] + 128 * 128 * digits[:, 2]


def experts_stage(tokens, expert_hidden, routes, route_weight, expert_weight, targets):
    x, h = (lax.axis_index(X), lax.axis_index(CORE))
    rows, top = routes.shape
    width = expert_hidden.shape[2] // 2
    cols = tokens.shape[1] // 2
    blocks = rows // 16
    by_block = routes.reshape(blocks, 16 * top).T
    mine = (by_block[:, :, None] == (lax.iota(jnp.int32, 16) * 4 + x)[None, None, :]).astype(bf16)
    n = 16 * top
    lower = (lax.iota(jnp.int32, n)[:, None] > lax.iota(jnp.int32, n)[None, :]).astype(bf16)
    before = dot(lower, mine.reshape(n, blocks * 16)).reshape(n, blocks, 16)
    slot = jnp.sum(before * mine.astype(f32), axis=2).astype(jnp.int32)
    place = by_block // 4 * 24 + lax.iota(jnp.int32, blocks)[None, :] * 3 + slot
    place = jnp.where(by_block % 4 == x, place, -1).T.reshape(rows, top)
    select = (lax.iota(jnp.int32, 384)[:, None] == place.reshape(-1)[None, :]).astype(bf16)
    hidden = lax.dynamic_slice_in_dim(
        expert_hidden.reshape(rows * top, 2 * width), h * width, width, 1
    )
    buffer = dot(select, hidden).astype(bf16).reshape(16, 24, width)
    extra = jnp.pad(label_row(targets), ((0, 7), (0, 0)))
    buffer = jnp.concatenate([buffer, jnp.broadcast_to(extra[None], (16, 8, width))], axis=1)
    received = lax.all_to_all(buffer, DP, 0, 0, tiled=True)
    labels = labels_of(received[:, 24])
    own = received[:, :24].reshape(384, width)
    other = swap_cores(own)
    weight = expert_weight[0]
    weight_own = lax.dynamic_slice_in_dim(weight, h * cols, cols, 1)
    weight_other = swap_cores(lax.dynamic_slice_in_dim(weight, (1 - h) * cols, cols, 1))
    product = (dot(own, weight_own) + dot(other, weight_other)).astype(bf16)
    back = lax.all_to_all(product.reshape(16, 24, cols), DP, 0, 0, tiled=True)
    gate = jnp.sum(
        jnp.where(
            place[:, :, None] == lax.iota(jnp.int32, 384)[None, None, :],
            route_weight[:, :, None],
            0.0,
        ),
        axis=1,
    )
    gate_high = gate.astype(bf16)
    gate_low = (gate - gate_high.astype(f32)).astype(bf16)
    both = dot(jnp.concatenate([gate_high, gate_low]), back.reshape(384, cols))
    partial = (both[:rows] + both[rows:]).astype(bf16)
    parts = lax.all_to_all(partial.reshape(4, rows // 4, cols), X, 0, 0, tiled=True)
    moe = jnp.sum(parts.astype(f32), axis=0)
    mine_tokens = lax.dynamic_slice(tokens, (x * (rows // 4), h * cols), (rows // 4, cols))
    return ((mine_tokens.astype(f32) + moe).astype(bf16), labels)


def combined(peaks, totals, picks):
    peak = jnp.max(peaks, axis=0)
    return (peak, jnp.sum(totals * jnp.exp(peaks - peak), axis=0), jnp.sum(picks, axis=0))


def per_device(
    tokens,
    expert_hidden,
    routes,
    route_weight,
    expert_weight,
    norm_gain,
    head_weight,
    targets,
    rollout_logprob,
    advantages,
):
    h = lax.axis_index(CORE)
    tile, labels = experts_stage(
        tokens, expert_hidden, routes, route_weight, expert_weight, targets
    )
    sub, cols = (tile.shape[0] // 2, tile.shape[1])
    kept = lax.dynamic_slice_in_dim(tile, h * sub, sub, 0)
    got = swap_cores(lax.dynamic_slice_in_dim(tile, (1 - h) * sub, sub, 0))
    layer_sub = jnp.where(
        h == 0, jnp.concatenate([kept, got], axis=1), jnp.concatenate([got, kept], axis=1)
    )
    group_layer = lax.all_to_all(
        jnp.broadcast_to(layer_sub[None], (8, *layer_sub.shape)), VOCAB, 0, 0, tiled=True
    ).reshape(tokens.shape)
    widened = layer_sub.astype(f32)
    mean_square = jnp.mean(widened * widened, axis=-1, keepdims=True)
    normed_sub = (widened * lax.rsqrt(mean_square + norm_epsilon) * norm_gain).astype(bf16)
    voc_dev = head_weight.shape[1]
    columns = lax.axis_index(DP_VOCAB) * voc_dev + lax.iota(jnp.int32, voc_dev)
    by_device = labels.reshape(-1, 2, sub // 2)
    stats = []
    for c in range(2):
        piece = normed_sub[c * (sub // 2) : (c + 1) * (sub // 2)]
        normed = lax.all_gather(piece, DP_VOCAB, axis=0, tiled=True)
        logits = dot(normed, head_weight)
        peak = jnp.max(logits, axis=1)
        total = jnp.sum(jnp.exp(logits - peak[:, None]), axis=1)
        wanted = by_device[:, c].reshape(-1)
        picked = jnp.sum(jnp.where(columns[None, :] == wanted[:, None], logits, 0.0), axis=1)
        stats.append(jnp.stack([peak, total, picked]).reshape(3, -1, 1, sub // 2))
    stats = jnp.concatenate(stats, axis=2).reshape(3, 16, -1).transpose(1, 0, 2)
    sent = lax.all_to_all(stats, DP, 0, 0, tiled=True)
    group = jnp.stack(combined(sent[:, 0], sent[:, 1], sent[:, 2]))
    sent = lax.all_gather(group, VOCAB, axis=0)
    peak, total, target_logit = combined(sent[:, 0], sent[:, 1], sent[:, 2])
    token_logprob = target_logit - (peak + jnp.log(total))
    token_loss = clipped_loss(token_logprob, rollout_logprob, advantages)
    return (group_layer, token_logprob, token_loss)


def solution(mesh):
    torus = Mesh(mesh.devices.reshape(4, 4, 4, 2), ("dp_0", "dp_1", "vocab_0", "vocab_1"))
    placed = (
        P(DP, None),
        P(DP, None, None),
        P(DP, None),
        P(DP, None),
        P(DP_VOCAB, None, None),
        P(),
        P(None, DP_VOCAB),
        P(DP),
        P(DP),
        P(DP),
    )
    return jax.shard_map(
        per_device,
        mesh=torus,
        in_specs=placed,
        out_specs=(P(DP, None), P(DP), P(DP)),
        check_vma=False,
    )
```

profile of v0, /device:TPU:1, one launch (start us, length us, event | category | flops | bytes accessed | tf_op | source)
XLA Modules:
  0.0 330.1 jit_solution(12316371568212583948)
XLA Ops:
  7.2 4.3 %dynamic-slice_bitcast_fusion = bf16[512,3584]{1,0:T(8,128)(2,1)} fusion(bf16[1,512,7168]{2,1,0:T(8,128)(2,1)} %param.14, s32[]{:T(128)S(6)} %select_n.101), kind=kLoop, calls=%fused_computation.8 | loop fusion | bytes 7340036 | tf_op jit(solution)/shard_map/dynamic_slice | solution.py:75
  11.5 1.4 collective-permute-start.1
  13.6 0.6 fusion.6
  14.2 17.8 %all_to_all.25 = bf16[16,32,512]{2,1,0:T(8,128)(2,1)S(1)} all-to-all(bf16[16,32,512]{2,1,0:T(8,128)(2,1)S(1)} %pad_maximum_fusion), channel_id=1, replica_groups=mesh['dp_0'=4,'dp_1'=4,'vocab_0'=4,'vocab_1'=2] {'dp_0','dp_1'}, dimensions={0} | all-to-all | bytes 1048576 | tf_op jit(solution)/shard_map/all_to_all | solution.py:69
  32.1 2.4 collective-permute-start
  34.5 3.6 %fusion.1 = f32[384,3584]{1,0:T(8,128)S(1)} fusion(bf16[384,512]{1,0:T(8,128)(2,1)S(1)} %bitcast.58, bf16[1,512,7168]{2,1,0:T(8,128)(2,1)} %param.14, s32[]{:T(128)S(6)} %select_n.90), kind=kOutput, calls=%fused_computation.2 | convolution fusion | flops 1409286144 | bytes 9568260 | tf_op jit(solution)/shard_map/dot_general | solution.py:30
  38.1 5.2 %fusion = bf16[384,3584]{1,0:T(8,128)(2,1)} fusion(f32[384,3584]{1,0:T(8,128)S(1)} %fusion.1, bf16[384,512]{1,0:T(8,128)(2,1)S(1)} %collective-permute-done, bf16[512,3584]{1,0:T(8,128)(2,1)} %collective-permute-done.1), kind=kOutput, calls=%fused_computation.1 | convolution fusion | flops 1412038656 | bytes 12320768 | tf_op jit(solution)/shard_map/dot_general | solution.py:30
  43.3 3.9 %all-to-all-start.1 = ((bf16[16,24,3584]{2,1,0:T(8,128)(2,1)}), bf16[16,24,3584]{2,1,0:T(8,128)(2,1)S(1)}, u32[]{:S(2)}, u32[]{:S(2)}) async-start(bf16[16,24,3584]{2,1,0:T(8,128)(2,1)} %bitcast.56), calls=%async_computation.1 | async-start | bytes 5505024 | tf_op jit(solution)/shard_map/all_to_all | solution.py:77
  47.4 0.5 select_reduce_fusion.2
  48.0 36.7 %all-to-all-done.1 = bf16[16,24,3584]{2,1,0:T(8,128)(2,1)S(1)} async-done(((bf16[16,24,3584]{2,1,0:T(8,128)(2,1)}), bf16[16,24,3584]{2,1,0:T(8,128)(2,1)S(1)}, u32[]{:S(2)}, u32[]{:S(2)}) %all-to-all-start.1) | async-done | bytes 2752544 | tf_op jit(solution)/shard_map/all_to_all | solution.py:77
  84.7 1.1 fusion.13
  85.8 1.1 fusion.4
  86.9 4.1 %all-to-all-start.2 = ((bf16[4,32,3584]{2,1,0:T(8,128)(2,1)}), bf16[4,32,3584]{2,1,0:T(8,128)(2,1)S(1)}, u32[]{:S(2)}, u32[]{:S(2)}) async-start(bf16[4,32,3584]{2,1,0:T(8,128)(2,1)} %bitcast.17), calls=%async_computation.2 | async-start | bytes 1835008 | tf_op jit(solution)/shard_map/all_to_all | solution.py:90
  91.0 12.0 %all-to-all-done.2 = bf16[4,32,3584]{2,1,0:T(8,128)(2,1)S(1)} async-done(((bf16[4,32,3584]{2,1,0:T(8,128)(2,1)}), bf16[4,32,3584]{2,1,0:T(8,128)(2,1)S(1)}, u32[]{:S(2)}, u32[]{:S(2)}) %all-to-all-start.2) | async-done | bytes 917536 | tf_op jit(solution)/shard_map/all_to_all | solution.py:90
  103.2 1.0 add_convert_fusion
  104.2 2.7 collective-permute-start.2
  106.9 1.0 collective-permute-done.2
  108.2 0.7 fusion.42
  109.0 0.7 all-gather.7.cloned.1.call-update
  110.6 1.4 broadcast_in_dim.25
  112.0 4.6 %all-to-all-start.3 = ((bf16[8,16,7168]{2,1,0:T(8,128)(2,1)}), bf16[8,16,7168]{2,1,0:T(8,128)(2,1)}, u32[]{:S(2)}, u32[]{:S(2)}) async-start(bf16[8,16,7168]{2,1,0:T(8,128)(2,1)} %broadcast_in_dim.25), calls=%async_computation.3 | async-start | bytes 3670016 | tf_op jit(solution)/shard_map/all_to_all | solution.py:123
  116.6 71.4 %all-gather.5.cloned.1.call-done = bf16[1024,7168]{1,0:T(8,128)(2,1)} async-done(((bf16[8,7168]{1,0:T(8,128)(2,1)}), bf16[1024,7168]{1,0:T(8,128)(2,1)}) %all-gather.5.cloned.1.call-update) | async-done | bytes 14680080 | tf_op jit(solution)/shard_map/all_gather | solution.py:135
  188.0 20.6 %fusion.44 = (f32[1024]{0:T(1024)S(1)}, f32[1024,896]{0,1:T(8,128)}) fusion(bf16[1024,7168]{1,0:T(8,128)(2,1)} %all-gather.5.cloned.1.call-done, bf16[7168,896]{1,0:T(8,128)(2,1)} %param.16), kind=kOutput, calls=%fused_computation.106 | convolution fusion | flops 13154253824 | bytes 31199232 | tf_op jit(solution)/shard_map/dot_general | solution.py:30
  208.7 58.5 %all-gather.7.cloned.1.call-done = bf16[1024,7168]{1,0:T(8,128)(2,1)} async-done(((bf16[8,7168]{1,0:T(8,128)(2,1)}), bf16[1024,7168]{1,0:T(8,128)(2,1)}) %all-gather.7.cloned.1.call-update) | async-done | bytes 14680080 | tf_op jit(solution)/shard_map/all_gather | solution.py:135
  267.2 20.9 %fusion.45 = (f32[1024]{0:T(1024)S(1)}, f32[1024,896]{0,1:T(8,128)}) fusion(bf16[1024,7168]{1,0:T(8,128)(2,1)} %all-gather.7.cloned.1.call-done, bf16[7168,896]{1,0:T(8,128)(2,1)} %param.16), kind=kOutput, calls=%fused_computation.107 | convolution fusion | flops 13154253824 | bytes 31199232 | tf_op jit(solution)/shard_map/dot_general | solution.py:30
  288.3 4.3 %exponential_reduce_fusion.1 = (f32[1024]{0:T(1024)S(1)}, f32[1024]{0:T(1024)S(1)}, f32[1024]{0:T(1024)S(1)}, f32[1024]{0:T(1024)S(1)}) fusion(f32[1024,896]{0,1:T(8,128)} %get-tuple-element.32, f32[1024]{0:T(1024)S(1)} %get-tuple-element.31, s32[1024]{0:T(1024)S(1)} %eq.118, s32[896]{0:T(1024)S(1)} %iota_add_fusion, f32[1024,896]{0,1:T(8,128)} %get-tuple-element.34, ...), kind=kLoop, calls=%fused_computation.7 | loop fusion | flops 9170944 | bytes 7376384 | tf_op jit(solution)/shard_map/reduce_sum | solution.py:138
  294.1 0.6 copy.49
  294.7 5.7 %all-to-all-start.4 = ((f32[16,3,128]{2,1,0:T(4,128)}), f32[16,3,128]{2,1,0:T(4,128)S(1)}, u32[]{:S(2)}, u32[]{:S(2)}) async-start(f32[16,3,128]{2,1,0:T(4,128)} %copy.49), calls=%async_computation.4 | async-start | bytes 65536 | tf_op jit(solution)/shard_map/all_to_all | solution.py:143
  300.5 6.5 %all-to-all-done.4 = f32[16,3,128]{2,1,0:T(4,128)S(1)} async-done(((f32[16,3,128]{2,1,0:T(4,128)}), f32[16,3,128]{2,1,0:T(4,128)S(1)}, u32[]{:S(2)}, u32[]{:S(2)}) %all-to-all-start.4) | async-done | bytes 24608 | tf_op jit(solution)/shard_map/all_to_all | solution.py:143
  307.0 12.8 %all-gather.1 = f32[8,3,128]{2,1,0:T(4,128)S(1)} all-gather(f32[1,3,128]{2,1,0:T(4,128)S(1)} %maximum_bitcast_fusion), channel_id=2, replica_groups=mesh['dp_0'=4,'dp_1'=4,'vocab_0'=4,'vocab_1'=2] {'vocab_0','vocab_1'}, dimensions={0}, use_global_device_ids=true | all-gather | bytes 13824 | tf_op jit(solution)/shard_map/all_gather | solution.py:145
  319.9 0.5 fusion.40
  320.5 2.8 copy.55
  (75 shorter events, 4.2 us)
Async XLA Ops:
  7.2 6.4 %copy-start = (bf16[128,8,1024]{2,1,0:T(8,128)(2,1)S(1)}, bf16[128,8,1024]{2,1,0:T(8,128)(2,1)}, u32[]{:S(2)}) copy-start(bf16[128,8,1024]{2,1,0:T(8,128)(2,1)} %param.11) | copy-start | bytes 6291460
  7.2 5.8 %copy-start.7 = (s32[128]{0:T(128)S(1)}, s32[128]{0:T(128)}, u32[]{:S(2)}) copy-start(s32[128]{0:T(128)} %param.17) | copy-start | bytes 1540
  7.2 5.8 %copy-start.3 = (s32[128,8]{0,1:T(8,128)S(1)}, s32[128,8]{0,1:T(8,128)}, u32[]{:S(2)}) copy-start(s32[128,8]{0,1:T(8,128)} %param.12) | copy-start | bytes 12292
  11.5 26.7 %collective-permute-start.1 = (bf16[512,3584]{1,0:T(8,128)(2,1)}, bf16[512,3584]{1,0:T(8,128)(2,1)}, u32[]{:S(2)}, u32[]{:S(2)}) collective-permute-start(bf16[512,3584]{1,0:T(8,128)(2,1)} %dynamic-slice_bitcast_fusion), channel_id=1, source_target_pairs={{0,1},{1,0},{2,3},{3,2},{4,5},{5,4},{6,7},{7,6},{8,9},{9,8},{10,11... | collective-permute-start | bytes 11010056 | tf_op jit(solution)/shard_map/ppermute | solution.py:34
  32.1 6.0 %collective-permute-start = (bf16[384,512]{1,0:T(8,128)(2,1)S(1)}, bf16[384,512]{1,0:T(8,128)(2,1)S(1)}, u32[]{:S(2)}, u32[]{:S(2)}) collective-permute-start(bf16[384,512]{1,0:T(8,128)(2,1)S(1)} %bitcast.57), channel_id=1, source_target_pairs={{0,1},{1,0},{2,3},{3,2},{4,5},{5,4},{6,7},{7,6},{8,9},{9,8},{10,11... | collective-permute-start | bytes 1179656 | tf_op jit(solution)/shard_map/ppermute | solution.py:34
  43.3 4.0 %copy-start.4 = (f32[128,8]{0,1:T(8,128)S(1)}, f32[128,8]{0,1:T(8,128)}, u32[]{:S(2)}) copy-start(f32[128,8]{0,1:T(8,128)} %param.13) | copy-start | bytes 12292
  43.3 41.4 %all-to-all-start.1 = ((bf16[16,24,3584]{2,1,0:T(8,128)(2,1)}), bf16[16,24,3584]{2,1,0:T(8,128)(2,1)S(1)}, u32[]{:S(2)}, u32[]{:S(2)}) async-start(bf16[16,24,3584]{2,1,0:T(8,128)(2,1)} %bitcast.56), calls=%async_computation.1 | async-start | bytes 5505024 | tf_op jit(solution)/shard_map/all_to_all | solution.py:77
  86.9 21.2 %copy-start.2 = (f32[7168]{0:T(1024)S(1)}, f32[7168]{0:T(1024)}, u32[]{:S(2)}) copy-start(f32[7168]{0:T(1024)} %param.15) | copy-start | bytes 86020
  86.9 16.2 %all-to-all-start.2 = ((bf16[4,32,3584]{2,1,0:T(8,128)(2,1)}), bf16[4,32,3584]{2,1,0:T(8,128)(2,1)S(1)}, u32[]{:S(2)}, u32[]{:S(2)}) async-start(bf16[4,32,3584]{2,1,0:T(8,128)(2,1)} %bitcast.17), calls=%async_computation.2 | async-start | bytes 1835008 | tf_op jit(solution)/shard_map/all_to_all | solution.py:90
  91.0 97.0 %all-gather.5.cloned.1.call-start = ((), (), s32[]{:S(2)}) async-start(), calls=%async_computation.5 | async-start | bytes 14794752 | tf_op jit(solution)/shard_map/all_gather | solution.py:135
  104.2 3.7 %collective-permute-start.2 = (bf16[16,3584]{1,0:T(8,128)(2,1)S(1)}, bf16[16,3584]{1,0:T(8,128)(2,1)S(1)}, u32[]{:S(2)}, u32[]{:S(2)}) collective-permute-start(bf16[16,3584]{1,0:T(8,128)(2,1)S(1)} %get-tuple-element.19), channel_id=1, source_target_pairs={{0,1},{1,0},{2,3},{3,2},{4,5},{5,4},{6,7},{7,6},{8,9},{9,8},{10,11... | collective-permute-start | bytes 344072 | tf_op jit(solution)/shard_map/ppermute | solution.py:34
  109.0 158.2 %all-gather.7.cloned.1.call-start = ((), (), s32[]{:S(2)}) async-start(), calls=%async_computation.6 | async-start | bytes 14794752 | tf_op jit(solution)/shard_map/all_gather | solution.py:135
  112.0 182.7 %all-to-all-start.3 = ((bf16[8,16,7168]{2,1,0:T(8,128)(2,1)}), bf16[8,16,7168]{2,1,0:T(8,128)(2,1)}, u32[]{:S(2)}, u32[]{:S(2)}) async-start(bf16[8,16,7168]{2,1,0:T(8,128)(2,1)} %broadcast_in_dim.25), calls=%async_computation.3 | async-start | bytes 3670016 | tf_op jit(solution)/shard_map/all_to_all | solution.py:123
  288.3 31.6 %copy-start.5 = (f32[128]{0:T(128)S(1)}, f32[128]{0:T(128)}, u32[]{:S(2)}) copy-start(f32[128]{0:T(128)} %param.19) | copy-start | bytes 1540
  288.3 31.6 %copy-start.6 = (f32[128]{0:T(128)S(1)}, f32[128]{0:T(128)}, u32[]{:S(2)}) copy-start(f32[128]{0:T(128)} %param.18) | copy-start | bytes 1540
  288.3 35.0 %copy-start.1 = (bf16[128,8,1024]{2,1,0:T(8,128)(2,1)S(1)}, bf16[128,8,1024]{2,1,0:T(8,128)(2,1)}, u32[]{:S(2)}) copy-start(bf16[128,8,1024]{2,1,0:T(8,128)(2,1)} %param.11) | copy-start | bytes 6291460
  294.7 12.2 %all-to-all-start.4 = ((f32[16,3,128]{2,1,0:T(4,128)}), f32[16,3,128]{2,1,0:T(4,128)S(1)}, u32[]{:S(2)}, u32[]{:S(2)}) async-start(f32[16,3,128]{2,1,0:T(4,128)} %copy.49), calls=%async_computation.4 | async-start | bytes 65536 | tf_op jit(solution)/shard_map/all_to_all | solution.py:143
Sparse Core Ops, SparseCore 0:
  109.1 78.8 all-gather.4
  191.0 76.1 all-gather.6
where the time goes:
time: 331 us; the launch traced here: 330 us
  waiting for transfers between devices  187 us (56%)
  matrix products  52.2 us (16%)
  blocking collectives  30.6 us (9%)
  starting transfers between devices  24.8 us (7%)
  between operations  14.4 us (4%)
  local copies, waits for them, and re-layouts  12.8 us (4%)
  other arithmetic  8.41 us (3%)
    all_gather x2, waiting for transfers between devices, per_device(): normed = lax.all_gather(piece, DP_VOCAB, axis=0, tiled=True)  130 us
    dot_general x7, matrix products, dot(): return jnp.dot(a, b, preferred_element_type=f32)  52.2 us
    all_to_all x1, waiting for transfers between devices, experts_stage(): back = lax.all_to_all(product.reshape(16, 24, cols), DP, 0, 0, tiled=True)  36.7 us
    all_to_all x1, blocking collectives, experts_stage(): received = lax.all_to_all(buffer, DP, 0, 0, tiled=True)  17.8 us
    all_gather x1, blocking collectives, per_device(): sent = lax.all_gather(group, VOCAB, axis=0)  12.8 us
    all_to_all x1, waiting for transfers between devices, experts_stage(): lax.all_to_all(partial.reshape(4, rows // 4, cols), X, 0, 0, tiled=True)  12 us
  transfers between devices with their start and end apart: 9, of which 6 were waited for; matrix products, arithmetic and copies ran while one was open for 17% of the time, Pallas kernels for 0%

commit v1 on v0

--- a/solution.py
+++ b/solution.py
@@ -132,7 +132,10 @@
     stats = []
     for c in range(2):
         piece = normed_sub[c * (sub // 2) : (c + 1) * (sub // 2)]
-        normed = lax.all_gather(piece, DP_VOCAB, axis=0, tiled=True)
+        n_dev = lax.axis_size(DP_VOCAB)
+        pieces = jnp.stack([piece for _ in range(n_dev)])
+        pieces = lax.all_to_all(pieces, DP_VOCAB, split_axis=0, concat_axis=0)
+        normed = jnp.concatenate(pieces, axis=0)
         logits = dot(normed, head_weight)
         peak = jnp.max(logits, axis=1)
         total = jnp.sum(jnp.exp(logits - peak[:, None]), axis=1)

time: 331 us -> 564 us (1.70)
  blocking collectives: 30.6 us -> 207 us
  waiting for transfers between devices: 187 us -> 232 us
  local copies, waits for them, and re-layouts: 12.8 us -> 26.2 us
  between operations: 14.4 us -> 1.05 us
  starting transfers between devices: 24.8 us -> 34.7 us
    all_to_all x0 -> x1, waiting for transfers between devices: none -> 176 us  [per_device(): pieces = lax.all_to_all(pieces, DP_VOCAB, split_axis=0, concat_axis=0)]
    all_to_all x0 -> x1, blocking collectives: none -> 175 us  [per_device(): pieces = lax.all_to_all(pieces, DP_VOCAB, split_axis=0, concat_axis=0)]
    all_gather x2 -> x0, waiting for transfers between devices: 130 us -> none  [per_device(): normed = lax.all_gather(piece, DP_VOCAB, axis=0, tiled=True)]
    another operation x0 -> x2, local copies, waits for them, and re-layouts: none -> 14.1 us  [per_device(): pieces = jnp.stack([piece for _ in range(n_dev)])]
    all_to_all x0 -> x1, starting transfers between devices: none -> 9.05 us  [per_device(): pieces = lax.all_to_all(pieces, DP_VOCAB, split_axis=0, concat_axis=0)]
  transfers between devices with their start and end apart: 9 -> 8, of which waited for: 6 -> 5; matrix products, arithmetic and copies ran while one was open for 17% -> 10% of each run, Pallas kernels for 0% -> 0%
where the time goes in v1:
time: 564 us; the launch traced here: 563 us
  waiting for transfers between devices  232 us (41%)
  blocking collectives  207 us (37%)
  matrix products  53.8 us (10%)
  starting transfers between devices  34.7 us (6%)
  local copies, waits for them, and re-layouts  26.2 us (5%)
  other arithmetic  8.41 us (1%)
    all_to_all x1, waiting for transfers between devices, per_device(): pieces = lax.all_to_all(pieces, DP_VOCAB, split_axis=0, concat_axis=0)  176 us
    all_to_all x1, blocking collectives, per_device(): pieces = lax.all_to_all(pieces, DP_VOCAB, split_axis=0, concat_axis=0)  175 us
    dot_general x7, matrix products, dot(): return jnp.dot(a, b, preferred_element_type=f32)  53.8 us
    all_to_all x1, waiting for transfers between devices, experts_stage(): back = lax.all_to_all(product.reshape(16, 24, cols), DP, 0, 0, tiled=True)  36.8 us
    all_to_all x1, blocking collectives, experts_stage(): received = lax.all_to_all(buffer, DP, 0, 0, tiled=True)  17.8 us
    another operation x2, local copies, waits for them, and re-layouts, per_device(): pieces = jnp.stack([piece for _ in range(n_dev)])  14.1 us
    all_gather x1, blocking collectives, per_device(): sent = lax.all_gather(group, VOCAB, axis=0)  13.8 us
    all_to_all x1, waiting for transfers between devices, experts_stage(): lax.all_to_all(partial.reshape(4, rows // 4, cols), X, 0, 0, tiled=True)  12 us
  transfers between devices with their start and end apart: 8, of which 5 were waited for; matrix products, arithmetic and copies ran while one was open for 10% of the time, Pallas kernels for 0%

profile of v1, /device:TPU:1, one launch (start us, length us, event | category | flops | bytes accessed | tf_op | source)
XLA Modules:
  0.0 563.3 jit_solution(16420926928310033634)
XLA Ops:
  0.7 4.3 dynamic-slice_bitcast_fusion
  4.9 1.4 collective-permute-start.1
  7.1 0.6 fusion.10
  7.7 17.8 %all_to_all.35 = bf16[16,32,512]{2,1,0:T(8,128)(2,1)S(1)} all-to-all(bf16[16,32,512]{2,1,0:T(8,128)(2,1)S(1)} %pad_maximum_fusion), channel_id=1, replica_groups=mesh['dp_0'=4,'dp_1'=4,'vocab_0'=4,'vocab_1'=2] {'dp_0','dp_1'}, dimensions={0} | all-to-all | bytes 1048576 | tf_op jit(solution)/shard_map/all_to_all | solution.py:69
  25.6 2.4 collective-permute-start
  28.0 3.6 fusion.5
  31.6 5.2 fusion.4
  36.8 4.6 all-to-all-start.1
  42.2 36.8 %all-to-all-done.1 = bf16[16,24,3584]{2,1,0:T(8,128)(2,1)} async-done(((bf16[16,24,3584]{2,1,0:T(8,128)(2,1)}), bf16[16,24,3584]{2,1,0:T(8,128)(2,1)}, u32[]{:S(2)}, u32[]{:S(2)}) %all-to-all-start.1) | async-done | bytes 2752544 | tf_op jit(solution)/shard_map/all_to_all | solution.py:77
  78.9 2.9 fusion.17
  81.8 1.1 fusion.8
  82.9 4.1 all-to-all-start.2
  87.1 12.0 %all-to-all-done.2 = bf16[4,32,3584]{2,1,0:T(8,128)(2,1)S(1)} async-done(((bf16[4,32,3584]{2,1,0:T(8,128)(2,1)}), bf16[4,32,3584]{2,1,0:T(8,128)(2,1)S(1)}, u32[]{:S(2)}, u32[]{:S(2)}) %all-to-all-start.2) | async-done | bytes 917536 | tf_op jit(solution)/shard_map/all_to_all | solution.py:90
  99.2 1.0 add_convert_fusion
  100.3 2.7 collective-permute-start.2
  102.9 1.0 collective-permute-done.2
  104.3 7.0 %stack.28 = bf16[128,8,7168]{2,1,0:T(8,128)(2,1)} broadcast(bf16[8,7168]{1,0:T(8,128)(2,1)S(1)} %get-tuple-element.17), dimensions={1,2} | broadcast | bytes 14794752 | tf_op jit(solution)/shard_map/stack | solution.py:136
  111.3 175.2 %all_to_all.36 = bf16[128,8,7168]{2,1,0:T(8,128)(2,1)} all-to-all(bf16[128,8,7168]{2,1,0:T(8,128)(2,1)} %stack.28), channel_id=1, replica_groups=mesh['dp_0'=4,'dp_1'=4,'vocab_0'=4,'vocab_1'=2] {'dp_0','dp_1','vocab_0'..., dimensions={0} | all-to-all | bytes 29360128 | tf_op jit(solution)/shard_map/all_to_all | solution.py:137
  286.6 7.0 %stack.33 = bf16[128,8,7168]{2,1,0:T(8,128)(2,1)} broadcast(bf16[8,7168]{1,0:T(8,128)(2,1)S(1)} %get-tuple-element.18), dimensions={1,2} | broadcast | bytes 14794752 | tf_op jit(solution)/shard_map/stack | solution.py:136
  293.6 9.0 %all-to-all-start.5 = ((bf16[128,8,7168]{2,1,0:T(8,128)(2,1)}), bf16[128,8,7168]{2,1,0:T(8,128)(2,1)}, u32[]{:S(2)}, u32[]{:S(2)}) async-start(bf16[128,8,7168]{2,1,0:T(8,128)(2,1)} %stack.33), calls=%async_computation.5 | async-start | bytes 29360128 | tf_op jit(solution)/shard_map/all_to_all | solution.py:137
  303.6 20.8 %fusion.48 = (f32[1024]{0:T(1024)S(1)}, f32[1024,896]{0,1:T(8,128)}) fusion(bf16[7168,896]{1,0:T(8,128)(2,1)} %param.16, bf16[128,8,7168]{2,1,0:T(8,128)(2,1)} %all_to_all.36), kind=kOutput, calls=%fused_computation.110 | convolution fusion | flops 13154253824 | bytes 31199232 | tf_op jit(solution)/shard_map/dot_general | solution.py:30
  324.3 176.1 %all-to-all-done.5 = bf16[128,8,7168]{2,1,0:T(8,128)(2,1)} async-done(((bf16[128,8,7168]{2,1,0:T(8,128)(2,1)}), bf16[128,8,7168]{2,1,0:T(8,128)(2,1)}, u32[]{:S(2)}, u32[]{:S(2)}) %all-to-all-start.5) | async-done | bytes 14680096 | tf_op jit(solution)/shard_map/all_to_all | solution.py:137
  500.4 1.4 broadcast_in_dim.25
  501.8 7.0 %all-to-all-start.3 = ((bf16[8,16,7168]{2,1,0:T(8,128)(2,1)}), bf16[8,16,7168]{2,1,0:T(8,128)(2,1)}, u32[]{:S(2)}, u32[]{:S(2)}) async-start(bf16[8,16,7168]{2,1,0:T(8,128)(2,1)} %broadcast_in_dim.25), calls=%async_computation.3 | async-start | bytes 3670016 | tf_op jit(solution)/shard_map/all_to_all | solution.py:123
  508.8 20.6 %fusion.49 = (f32[1024]{0:T(1024)S(1)}, f32[1024,896]{0,1:T(8,128)}) fusion(bf16[7168,896]{1,0:T(8,128)(2,1)} %param.16, bf16[128,8,7168]{2,1,0:T(8,128)(2,1)} %all-to-all-done.5), kind=kOutput, calls=%fused_computation.111 | convolution fusion | flops 13154253824 | bytes 31199232 | tf_op jit(solution)/shard_map/dot_general | solution.py:30
  529.6 4.3 exponential_reduce_fusion.1
  535.4 0.6 copy.49
  536.0 3.5 all-to-all-start.6
  539.5 6.4 %all-to-all-done.6 = f32[16,3,128]{2,1,0:T(4,128)S(1)} async-done(((f32[16,3,128]{2,1,0:T(4,128)}), f32[16,3,128]{2,1,0:T(4,128)S(1)}, u32[]{:S(2)}, u32[]{:S(2)}) %all-to-all-start.6) | async-done | bytes 24608 | tf_op jit(solution)/shard_map/all_to_all | solution.py:146
  546.1 13.8 %all-gather.1 = f32[8,3,128]{2,1,0:T(4,128)S(1)} all-gather(f32[1,3,128]{2,1,0:T(4,128)S(1)} %maximum_bitcast_fusion), channel_id=2, replica_groups=mesh['dp_0'=4,'dp_1'=4,'vocab_0'=4,'vocab_1'=2] {'vocab_0','vocab_1'}, dimensions={0}, use_global_device_ids=true | all-gather | bytes 13824 | tf_op jit(solution)/shard_map/all_gather | solution.py:148
  559.9 0.5 fusion.44
  560.5 2.8 copy.55
  (74 shorter events, 4.7 us)
Async XLA Ops:
  0.6 6.4 %copy-start = (bf16[128,8,1024]{2,1,0:T(8,128)(2,1)S(1)}, bf16[128,8,1024]{2,1,0:T(8,128)(2,1)}, u32[]{:S(2)}) copy-start(bf16[128,8,1024]{2,1,0:T(8,128)(2,1)} %param.11) | copy-start | bytes 6291460
  0.7 5.8 %copy-start.3 = (s32[128,8]{0,1:T(8,128)S(1)}, s32[128,8]{0,1:T(8,128)}, u32[]{:S(2)}) copy-start(s32[128,8]{0,1:T(8,128)} %param.12) | copy-start | bytes 12292
  0.7 6.0 %copy-start.7 = (s32[128]{0:T(128)S(1)}, s32[128]{0:T(128)}, u32[]{:S(2)}) copy-start(s32[128]{0:T(128)} %param.17) | copy-start | bytes 1540
  4.9 26.7 %collective-permute-start.1 = (bf16[512,3584]{1,0:T(8,128)(2,1)}, bf16[512,3584]{1,0:T(8,128)(2,1)}, u32[]{:S(2)}, u32[]{:S(2)}) collective-permute-start(bf16[512,3584]{1,0:T(8,128)(2,1)} %dynamic-slice_bitcast_fusion), channel_id=1, source_target_pairs={{0,1},{1,0},{2,3},{3,2},{4,5},{5,4},{6,7},{7,6},{8,9},{9,8},{10,11... | collective-permute-start | bytes 11010056 | tf_op jit(solution)/shard_map/ppermute | solution.py:34
  25.6 6.0 %collective-permute-start = (bf16[384,512]{1,0:T(8,128)(2,1)S(1)}, bf16[384,512]{1,0:T(8,128)(2,1)S(1)}, u32[]{:S(2)}, u32[]{:S(2)}) collective-permute-start(bf16[384,512]{1,0:T(8,128)(2,1)S(1)} %bitcast.64), channel_id=1, source_target_pairs={{0,1},{1,0},{2,3},{3,2},{4,5},{5,4},{6,7},{7,6},{8,9},{9,8},{10,11... | collective-permute-start | bytes 1179656 | tf_op jit(solution)/shard_map/ppermute | solution.py:34
  36.8 4.7 copy-start.4
  36.8 42.2 %all-to-all-start.1 = ((bf16[16,24,3584]{2,1,0:T(8,128)(2,1)}), bf16[16,24,3584]{2,1,0:T(8,128)(2,1)}, u32[]{:S(2)}, u32[]{:S(2)}) async-start(bf16[16,24,3584]{2,1,0:T(8,128)(2,1)} %bitcast.63), calls=%async_computation.1 | async-start | bytes 5505024 | tf_op jit(solution)/shard_map/all_to_all | solution.py:77
  82.9 21.2 %copy-start.2 = (f32[7168]{0:T(1024)S(1)}, f32[7168]{0:T(1024)}, u32[]{:S(2)}) copy-start(f32[7168]{0:T(1024)} %param.15) | copy-start | bytes 86020
  82.9 16.2 %all-to-all-start.2 = ((bf16[4,32,3584]{2,1,0:T(8,128)(2,1)}), bf16[4,32,3584]{2,1,0:T(8,128)(2,1)S(1)}, u32[]{:S(2)}, u32[]{:S(2)}) async-start(bf16[4,32,3584]{2,1,0:T(8,128)(2,1)} %bitcast.17), calls=%async_computation.2 | async-start | bytes 1835008 | tf_op jit(solution)/shard_map/all_to_all | solution.py:90
  100.3 3.7 collective-permute-start.2
  293.6 206.8 %all-to-all-start.5 = ((bf16[128,8,7168]{2,1,0:T(8,128)(2,1)}), bf16[128,8,7168]{2,1,0:T(8,128)(2,1)}, u32[]{:S(2)}, u32[]{:S(2)}) async-start(bf16[128,8,7168]{2,1,0:T(8,128)(2,1)} %stack.33), calls=%async_computation.5 | async-start | bytes 29360128 | tf_op jit(solution)/shard_map/all_to_all | solution.py:137
  501.8 34.2 %all-to-all-start.3 = ((bf16[8,16,7168]{2,1,0:T(8,128)(2,1)}), bf16[8,16,7168]{2,1,0:T(8,128)(2,1)}, u32[]{:S(2)}, u32[]{:S(2)}) async-start(bf16[8,16,7168]{2,1,0:T(8,128)(2,1)} %broadcast_in_dim.25), calls=%async_computation.3 | async-start | bytes 3670016 | tf_op jit(solution)/shard_map/all_to_all | solution.py:123
  529.6 30.3 %copy-start.5 = (f32[128]{0:T(128)S(1)}, f32[128]{0:T(128)}, u32[]{:S(2)}) copy-start(f32[128]{0:T(128)} %param.19) | copy-start | bytes 1540
  529.6 30.3 %copy-start.6 = (f32[128]{0:T(128)S(1)}, f32[128]{0:T(128)}, u32[]{:S(2)}) copy-start(f32[128]{0:T(128)} %param.18) | copy-start | bytes 1540
  529.6 33.7 %copy-start.1 = (bf16[128,8,1024]{2,1,0:T(8,128)(2,1)S(1)}, bf16[128,8,1024]{2,1,0:T(8,128)(2,1)}, u32[]{:S(2)}) copy-start(bf16[128,8,1024]{2,1,0:T(8,128)(2,1)} %param.11) | copy-start | bytes 6291460
  536.0 9.9 %all-to-all-start.6 = ((f32[16,3,128]{2,1,0:T(4,128)}), f32[16,3,128]{2,1,0:T(4,128)S(1)}, u32[]{:S(2)}, u32[]{:S(2)}) async-start(f32[16,3,128]{2,1,0:T(4,128)} %copy.49), calls=%async_computation.6 | async-start | bytes 65536 | tf_op jit(solution)/shard_map/all_to_all | solution.py:146
